TPU v7x, 32 devices: a whole 2x2x4 slice. The times are simulated.
32 devices in a mesh: slab: 4 (over y, core), pencil: 8 (over z, x).
Axes of the slice: x: 2, y: 2, z: 4, core: 2. Of those that a mesh axis runs over, the one named last changes fastest.
Arguments:
- density: float32 [128, 768, 512], P('pencil', None, 'slab'), may hold values from -6 to 6
- source: float32 [128, 768, 512], P('pencil', None, 'slab'), may hold values from -6 to 8
- coupling: float32 [3], replicated, may hold values from 0.25 to 2, as said below
- width_inverse: float32 [6, 128, 128], replicated, as said below
- height_inverse: float32 [1, 128, 128], replicated, as said below
- depth_inverse: float32 [4, 128, 128], replicated, as said below
Outputs:
- stepped: float32 [128, 768, 512], P('pencil', None, 'slab')
Inputs may be any that keep to these rules, and one draw needn't show every extreme that they name: coupling holds three positive coefficients. `width_inverse`: block i is the inverse of the i-th pivot block of the block LU factorization of the tridiagonal line matrix with diagonal 1 + 2 s and off-diagonals -s, s the matching coupling. `height_inverse`: as for width_inverse, for the height lines. `depth_inverse`: as for width_inverse, for the depth lines.
All inputs are finite; a program needn't handle non-finite values.
Results may differ from a plain program's by a relative error of at most 0.00027.
Values sent between devices are 32-bit elements; how exact they have to be, the bound alone decides.
A program may use at most 128 MiB of HBM per device.

v0:
```python
import jax
import jax.numpy as jnp
from jax import lax
from jax.sharding import PartitionSpec as P


def extended(value, sides, width):
    for axis, dim in sides:
        count, length = (lax.axis_size(axis), value.shape[dim])
        up = [(i, (i + 1) % count) for i in range(count - 1)]
        down = [(j, i) for i, j in up]
        last = lax.slice_in_dim(value, length - width, length, axis=dim)
        leading = lax.slice_in_dim(value, 0, width, axis=dim)
        before = lax.ppermute(last, axis, up)
        after = lax.ppermute(leading, axis, down)
        value = jnp.concatenate([before, value, after], axis=dim)
    return value


def entering(part, axis, combine, identity, reverse):
    count = lax.axis_size(axis)
    place = lax.axis_index(axis)
    ahead = count - 1 - place if reverse else place
    gathered = jax.tree.map(lambda a: lax.all_gather(a, axis), part)
    state = jax.tree.map(lambda a, e: jnp.zeros_like(a) + jnp.asarray(e, a.dtype), part, identity)

    def one(step, state):
        source = count - 1 - step if reverse else step
        return combine(
            state, jax.tree.map(lambda a: lax.dynamic_index_in_dim(a, source, 0, False), gathered)
        )

    return lax.fori_loop(0, ahead, one, state)


def solve_inner(rhs, inverses, strength):
    outer, length, inner = rhs.shape
    size = inverses.shape[1]
    count = length // size
    blocked = rhs.reshape(outer, count, size, inner)

    def forward(current, state):
        result, carry = state
        piece = lax.dynamic_index_in_dim(blocked, current, 1, keepdims=False)
        matrix = lax.dynamic_index_in_dim(inverses, current, 0, keepdims=False)
        value = jnp.einsum("pkq,jk->pjq", piece, matrix, precision=lax.Precision.HIGHEST)
        value = value + strength * matrix[:, 0][None, :, None] * carry[:, None, :]
        result = lax.dynamic_update_index_in_dim(result, value, current, 1)
        return (result, value[:, size - 1, :])

    start = (jnp.zeros_like(blocked), jnp.zeros((outer, inner), blocked.dtype))
    halfway, unused = lax.fori_loop(0, count, forward, start)

    def backward(step, state):
        result, carry = state
        current = count - 1 - step
        value = lax.dynamic_index_in_dim(result, current, 1, keepdims=False)
        matrix = lax.dynamic_index_in_dim(inverses, current, 0, keepdims=False)
        value = value + strength * matrix[:, size - 1][None, :, None] * carry[:, None, :]
        result = lax.dynamic_update_index_in_dim(result, value, current, 1)
        return (result, value[:, 0, :])

    final, unused = lax.fori_loop(
        0, count, backward, (halfway, jnp.zeros((outer, inner), blocked.dtype))
    )
    return final.reshape(outer, length, inner)


def affine_combine(earlier, later):
    return (later[0] * earlier[0], later[0] * earlier[1] + later[1])


def per_device(density, source, coupling, width_inverse, height_inverse, depth_inverse):
    padded = extended(density, (("slab", 2), ("pencil", 0)), 1)
    center = padded[1:-1, :, 1:-1]
    along_height = padded[2:, :, 1:-1] + padded[:-2, :, 1:-1] - 2.0 * center
    along_depth = padded[1:-1, :, 2:] + padded[1:-1, :, :-2] - 2.0 * center
    width_padded = jnp.pad(density, ((0, 0), (1, 1), (0, 0)))
    along_width = width_padded[:, 2:, :] + width_padded[:, :-2, :] - 2.0 * density
    explicit = (
        2.0 * (coupling[0] * along_width + coupling[1] * along_height + coupling[2] * along_depth)
        + source
    )
    width_step = solve_inner(explicit, width_inverse, coupling[0])
    piece = lax.all_to_all(width_step, "pencil", split_axis=1, concat_axis=0, tiled=True)
    height_step = solve_inner(
        piece.reshape(1, piece.shape[0], -1), height_inverse, coupling[1]
    ).reshape(piece.shape)
    size = depth_inverse.shape[1]
    strength = coupling[2]
    matrix = lax.dynamic_index_in_dim(depth_inverse, lax.axis_index("slab"), 0, keepdims=False)
    local_value = jnp.einsum("yxk,jk->yxj", height_step, matrix, precision=lax.Precision.HIGHEST)
    forward_factor = jnp.reshape(strength * matrix[size - 1, 0], (1, 1))
    unit = jnp.ones((1, 1), local_value.dtype)
    zero_rows = jnp.zeros(local_value.shape[:2], local_value.dtype)
    unused, carry_in = entering(
        (forward_factor, local_value[:, :, size - 1]),
        "slab",
        affine_combine,
        (unit, zero_rows),
        False,
    )
    forward_value = local_value + strength * matrix[:, 0][None, None, :] * carry_in[:, :, None]
    backward_factor = jnp.reshape(strength * matrix[0, size - 1], (1, 1))
    unused, carry_next = entering(
        (backward_factor, forward_value[:, :, 0]), "slab", affine_combine, (unit, zero_rows), True
    )
    depth_step = (
        forward_value + strength * matrix[:, size - 1][None, None, :] * carry_next[:, :, None]
    )
    increment = lax.all_to_all(depth_step, "pencil", split_axis=0, concat_axis=1, tiled=True)
    return density + increment


def solution(mesh):
    in_specs = (P("pencil", None, "slab"), P("pencil", None, "slab"), P(), P(), P(), P())
    out_specs = P("pencil", None, "slab")
    return jax.shard_map(
        per_device, mesh=mesh, in_specs=in_specs, out_specs=out_specs, check_vma=False
    )
```

profile of v0, /device:TPU:27, one launch (start us, length us, event | category | flops | bytes accessed | tf_op | source)
XLA Modules:
  0.0 497.8 jit_solution(8275019180080528345)
XLA Ops:
  0.0 11.2 %fusion.34 = (f32[16,768,1]{2,1,0:T(8,128)}, f32[16,768,1]{2,1,0:T(8,128)}) fusion(f32[16,768,128]{2,1,0:T(8,128)} %param.14), kind=kLoop, calls=%fused_computation.71 | loop fusion | bytes 196608 | tf_op jit(solution)/shard_map/slice | solution.py:13
  11.2 4.4 copy.70
  15.6 3.7 collective-permute-start
  19.3 4.4 copy.71
  25.7 4.0 copy.41
  29.7 3.9 copy.42
  41.1 13.5 %collective-permute-done.2 = f32[1,768,130]{1,0,2:T(1,128)S(1)} collective-permute-done((f32[1,768,130]{1,0,2:T(1,128)S(1)}, f32[1,768,130]{1,0,2:T(1,128)S(1)}, u32[]{:S(2)}, u32[]{:S(2)}) %collective-permute-start.2) | collective-permute-done | bytes 399392 | tf_op jit(solution)/shard_map/ppermute | solution.py:15
  55.7 30.9 %fusion.17 = f32[16,768,128]{2,1,0:T(8,128)} fusion(f32[16,768,128]{2,1,0:T(8,128)} %param.15, f32[16,768,128]{2,1,0:T(8,128)} %param.14, f32[16,768,1]{2,1,0:T(8,128)} %copy.41, f32[16,768,1]{2,1,0:T(8,128)} %copy.42, f32[1,768,130]{2,1,0:T(8,128)S(1)} %copy.46, f32[1,768,130]{2,1,0:T(8,128)S(1)} %copy.44, f32[]{:T(128)} %bitcast.16, f32[]{:T(128)} %bitcast.15, ...), kind=kLoop, calls=%fused_computation.35 | loop fusion | flops 34603008 | bytes 19771404 | tf_op jit(solution)/shard_map/add | solution.py:81
  86.6 24.1 %while.70 = (s32[]{:T(128)}, f32[16,6,128,128]{3,2,1,0:T(8,128)}, f32[16,128]{1,0:T(8,128)S(1)}, f32[6,128,128]{2,1,0:T(8,128)S(1)}, f32[16,6,128,128]{3,2,1,0:T(8,128)}, /*index=5*/f32[]{:T(128)}, s32[]{:T(128)}) while((s32[]{:T(128)}, f32[16,6,128,128]{3,2,1,0:T(8,128)}, f32[16,128]{1,0:T(8,128)S(1)}, f32[6,128,128]{2,1,0:T(8,128)S(1)}, ...), condition=%wide.region_1.2_spmd, body=%wide.region_0.1_spmd.sunk | while | flops 403177600 | bytes 3370069 | solution.py:52
  87.4 3.2 bitcast_dynamic-update-slice_fusion.2
  91.4 3.2 bitcast_dynamic-update-slice_fusion.2
  95.4 3.2 bitcast_dynamic-update-slice_fusion.2
  99.4 3.2 bitcast_dynamic-update-slice_fusion.2
  103.4 3.2 bitcast_dynamic-update-slice_fusion.2
  107.5 3.2 bitcast_dynamic-update-slice_fusion.2
  110.8 23.1 %while.71 = (s32[]{:T(128)}, f32[16,6,128,128]{3,2,1,0:T(8,128)}, f32[16,128]{1,0:T(8,128)S(1)}, f32[]{:T(128)}, f32[6,128,128]{2,1,0:T(8,128)S(1)}, /*index=5*/s32[]{:T(128)}, s32[]{:T(128)}, s32[]{:T(128)}, s32[]{:T(128)}) while((s32[]{:T(128)}, f32[16,6,128,128]{3,2,1,0:T(8,128)}, f32[16,128]{1,0:T(8,128)S(1)}, f32[]{:T(128)}, ...), condition=%wide.region_3.4_spmd, body=%wide.region_2.3_spmd.sunk | while | flops 528518 | bytes 5555867 | solution.py:63
  133.8 9.0 %copy.52 = f32[16,6,128,128]{3,0,2,1:T(8,128)} copy(f32[16,6,128,128]{3,2,1,0:T(8,128)} %get-tuple-element.414) | data formatting | bytes 12582912 | tf_op jit(solution)/shard_map/while | solution.py:63
  142.9 6.8 %all-to-all-start = ((f32[16,768,128]{2,0,1:T(8,128)}), f32[16,768,128]{2,0,1:T(8,128)}, u32[]{:S(2)}, u32[]{:S(2)}) async-start(f32[16,768,128]{2,0,1:T(8,128)} %bitcast.110), calls=%async_computation | async-start | bytes 12582912 | tf_op jit(solution)/shard_map/all_to_all | solution.py:85
  154.8 6.5 %all-reduce.3 = (f32[4]{0:T(128)S(1)}, f32[4]{0:T(128)S(1)}) all-reduce(f32[4]{0:T(128)S(1)} %dynamic-update-slice, f32[4]{0:T(128)S(1)} %dynamic-update-slice.1), channel_id=1, replica_groups=mesh['slab'=4,'pencil'=8] {'slab'}, use_global_device_ids=true, to_apply=%add.1 | all-reduce | flops 8 | bytes 64
  162.9 123.4 %all-to-all-done = f32[16,768,128]{2,0,1:T(8,128)} async-done(((f32[16,768,128]{2,0,1:T(8,128)}), f32[16,768,128]{2,0,1:T(8,128)}, u32[]{:S(2)}, u32[]{:S(2)}) %all-to-all-start) | async-done | bytes 6291488 | tf_op jit(solution)/shard_map/all_to_all | solution.py:85
  286.3 4.7 copy.54
  290.9 13.5 %fusion.9 = f32[12288,128]{1,0:T(8,128)S(1)} fusion(f32[16,8,96,128]{3,2,1,0:T(8,128)S(1)} %bitcast.107, f32[128]{0:T(128)S(1)} %get-tuple-element.498, f32[128]{0:T(128)S(1)} %get-tuple-element.497, f32[1,128,128]{2,1,0:T(8,128)S(1)} %copy-done.3), kind=kOutput, calls=%fused_computation.26 | convolution fusion | flops 2419064832 | bytes 12649472 | tf_op jit(solution)/shard_map/while/body/eval_jaxpr/pkq,jk->pjq/dot_general | solution.py:46
  304.4 6.4 %fusion.29 = f32[128,96,128]{0,2,1:T(8,128)S(1)} fusion(f32[128,96,128]{0,2,1:T(8,128)S(1)} %bitcast.108, f32[4,128,128]{2,1,0:T(8,128)S(1)} %copy-done, s32[]{:T(128)S(6)} %select_n.60), kind=kOutput, calls=%fused_computation.65 | convolution fusion | flops 2415919104 | bytes 12648452 | tf_op jit(solution)/shard_map/yxk,jk->yxj/dot_general | solution.py:92
  310.8 2.7 copy-done.1
  313.6 6.1 %all-gather = f32[512,96,1]{0,2,1:T(1,128)S(1)} all-gather(f32[128,96,1]{0,2,1:T(1,128)S(1)} %slice.140), channel_id=2, replica_groups=mesh['slab'=4,'pencil'=8] {'slab'}, dimensions={0}, use_global_device_ids=true | all-gather | bytes 245760 | tf_op jit(solution)/shard_map/all_gather | solution.py:24
  321.2 3.9 multiply_add_fusion.1
  325.2 8.6 %all-gather.1 = f32[512,96,1]{0,2,1:T(1,128)S(1)} all-gather(f32[128,96,1]{0,2,1:T(1,128)S(1)} %slice.143), channel_id=3, replica_groups=mesh['slab'=4,'pencil'=8] {'slab'}, dimensions={0}, use_global_device_ids=true | all-gather | bytes 245760 | tf_op jit(solution)/shard_map/all_gather | solution.py:24
  333.8 2.9 while.73
  336.8 7.1 %multiply_add_fusion = f32[128,96,128]{0,2,1:T(8,128)} fusion(f32[128,96]{0,1:T(8,128)S(1)} %copy.59, f32[128]{0:T(128)S(1)} %get-tuple-element.495, f32[128,96,128]{0,2,1:T(8,128)} %copy-done.1, f32[128,96]{0,1:T(8,128)S(1)} %copy.57, f32[128]{0:T(128)S(1)} %get-tuple-element.496), kind=kLoop, calls=%fused_computation.50 | loop fusion | flops 6291456 | bytes 12682240 | tf_op jit(solution)/shard_map/add | solution.py:109
  343.8 6.6 %copy.60 = f32[128,96,128]{2,1,0:T(8,128)} copy(f32[128,96,128]{0,2,1:T(8,128)} %multiply_add_fusion) | data formatting | bytes 12582912 | tf_op jit(solution)/shard_map/add | solution.py:109
  350.5 141.9 %all_to_all.33 = f32[128,96,128]{2,1,0:T(8,128)S(1)} all-to-all(f32[128,96,128]{2,1,0:T(8,128)} %copy.60), channel_id=1, replica_groups=mesh['slab'=4,'pencil'=8] {'pencil'}, dimensions={0} | all-to-all | bytes 12582912 | tf_op jit(solution)/shard_map/all_to_all | solution.py:111
  493.9 3.4 bitcast_add_fusion.2
  (120 shorter events, 49.4 us)
Async XLA Ops:
  0.0 149.7 %copy-start = (f32[4,128,128]{2,1,0:T(8,128)S(1)}, f32[4,128,128]{2,1,0:T(8,128)}, u32[]{:S(2)}) copy-start(f32[4,128,128]{2,1,0:T(8,128)} %param.19) | copy-start | bytes 786436
  15.6 10.1 %collective-permute-start = (f32[16,768,1]{1,0,2:T(8,128)S(1)}, f32[16,768,1]{1,0,2:T(8,128)S(1)}, u32[]{:S(2)}, u32[]{:S(2)}) collective-permute-start(f32[16,768,1]{1,0,2:T(8,128)S(1)} %copy.70), channel_id=1, source_target_pairs={{0,8},{8,16},{16,24},{1,9},{9,17},{17,25},{2,10},{10,18},{18,26},{... | collective-permute-start | bytes 147464 | tf_op jit(solution)/shard_map/ppermute | solution.py:14
  23.7 5.9 %collective-permute-start.1 = (f32[16,768,1]{1,0,2:T(8,128)S(1)}, f32[16,768,1]{1,0,2:T(8,128)S(1)}, u32[]{:S(2)}, u32[]{:S(2)}) collective-permute-start(f32[16,768,1]{1,0,2:T(8,128)S(1)} %copy.71), channel_id=1, source_target_pairs={{8,0},{16,8},{24,16},{9,1},{17,9},{25,17},{10,2},{18,10},{26,18},{... | collective-permute-start | bytes 147464 | tf_op jit(solution)/shard_map/ppermute | solution.py:15
  33.6 6.9 %copy-start.4 = (f32[3]{0:T(128)S(1)}, f32[3]{0:T(128)}, u32[]{:S(2)}) copy-start(f32[3]{0:T(128)} %param.16) | copy-start | bytes 40
  36.3 18.3 %collective-permute-start.2 = (f32[1,768,130]{1,0,2:T(1,128)S(1)}, f32[1,768,130]{1,0,2:T(1,128)S(1)}, u32[]{:S(2)}, u32[]{:S(2)}) collective-permute-start(f32[1,768,130]{1,0,2:T(1,128)S(1)} %copy.43), channel_id=1, source_target_pairs={{1,0},{2,1},{3,2},{4,3},{5,4},{6,5},{7,6},{9,8},{10,9},{11,10},{12... | collective-permute-start | bytes 1198088 | tf_op jit(solution)/shard_map/ppermute | solution.py:15
  39.0 16.2 %collective-permute-start.3 = (f32[1,768,130]{1,0,2:T(1,128)S(1)}, f32[1,768,130]{1,0,2:T(1,128)S(1)}, u32[]{:S(2)}, u32[]{:S(2)}) collective-permute-start(f32[1,768,130]{1,0,2:T(1,128)S(1)} %copy.45), channel_id=1, source_target_pairs={{0,1},{1,2},{2,3},{3,4},{4,5},{5,6},{6,7},{8,9},{9,10},{10,11},{11... | collective-permute-start | bytes 1198088 | tf_op jit(solution)/shard_map/ppermute | solution.py:14
  55.6 30.9 %copy-start.2 = (f32[6,128,128]{2,1,0:T(8,128)S(1)}, f32[6,128,128]{2,1,0:T(8,128)}, u32[]{:S(2)}) copy-start(f32[6,128,128]{2,1,0:T(8,128)} %param.17) | copy-start | bytes 1179652
  142.9 9.8 %copy-start.5 = (u32[32]{0:T(128)S(1)}, u32[32]{0:T(128)}, u32[]{:S(2)}) copy-start(u32[32]{0:T(128)} %constant.197) | copy-start | bytes 388
  142.9 19.1 %copy-start.3 = (f32[1,128,128]{2,1,0:T(8,128)S(1)}, f32[1,128,128]{2,1,0:T(8,128)}, u32[]{:S(2)}) copy-start(f32[1,128,128]{2,1,0:T(8,128)} %param.18) | copy-start | bytes 196612
  142.9 143.4 %all-to-all-start = ((f32[16,768,128]{2,0,1:T(8,128)}), f32[16,768,128]{2,0,1:T(8,128)}, u32[]{:S(2)}, u32[]{:S(2)}) async-start(f32[16,768,128]{2,0,1:T(8,128)} %bitcast.110), calls=%async_computation | async-start | bytes 12582912 | tf_op jit(solution)/shard_map/all_to_all | solution.py:85
  310.8 2.7 copy-start.1
  350.5 142.5 %slice-start = ((s8[6291456]{0:T(1024)(128)(4,1)}), s8[4194304]{0:T(1024)(128)(4,1)S(1)}, s32[]{:S(2)}) async-start(s8[6291456]{0:T(1024)(128)(4,1)} %bitcast.105), calls=%async_computation.2 | async-start | bytes 8388608
  492.3 1.6 slice-start.1
where the time goes:
time: 507 us; the launch traced here: 498 us
  blocking collectives  163 us (32%)
  waiting for transfers between devices  137 us (27%)
  other arithmetic  73.9 us (15%)
  local copies, waits for them, and re-layouts  64.7 us (13%)
  matrix products  39.3 us (8%)
  starting transfers between devices  16.1 us (3%)
    all_to_all x1, blocking collectives, per_device(): lax.all_to_all(depth_step, 'pencil', split_axis=0, concat_axis=1, tiled=T...  142 us
    all_to_all x1, waiting for transfers between devices, per_device(): lax.all_to_all(width_step, 'pencil', split_axis=1, concat_axis=0, tiled=T...  123 us
    dot_general x7, matrix products, forward(): jnp.einsum('pkq,jk->pjq', piece, matrix, precision=lax.Precision.HIGHEST)  32.9 us
    add x1, other arithmetic, per_device(): 2.0 * (coupling[0] * along_width + coupling[1] * along_height + coupling[...  30.9 us
    all_gather x2, blocking collectives, entering(): gathered = jax.tree.map(lambda a: lax.all_gather(a, axis), part)  14.7 us
    unnamed x23, local copies, waits for them, and re-layouts  14.6 us
    dynamic_slice x6, other arithmetic, backward(): value = lax.dynamic_index_in_dim(result, current, 1, keepdims=False)  14.4 us
    ppermute x2, waiting for transfers between devices, extended(): after = lax.ppermute(leading, axis, down)  13.5 us
  transfers between devices with their start and end apart: 5, of which 2 were waited for; matrix products, arithmetic and copies ran while one was open for 3% of the time, Pallas kernels for 0%

commit v1 on v0

v1 whole, which is shorter than its diff:
```python
import jax
import jax.numpy as jnp
from jax import lax
from jax.experimental import pallas as pl
from jax.experimental.pallas import tpu as pltpu
from jax.sharding import PartitionSpec as P

F32, BF16 = jnp.float32, jnp.bfloat16


def split(value):
    high = value.astype(BF16)
    return high, (value - high.astype(F32)).astype(BF16)


def split_outside(value):
    high = lax.reduce_precision(value, 8, 7)
    return high.astype(BF16), (value - high).astype(BF16)


def both(value, axis):
    return jnp.concatenate(split(value), axis=axis)


def dot(a, b, dims):
    return lax.dot_general(a, b, (dims, ((), ())), preferred_element_type=F32)


def ends_of(plane):
    depth = plane.shape[1]
    row = lax.broadcasted_iota(jnp.int32, (16, 2 * depth), 0)
    lane = lax.broadcasted_iota(jnp.int32, (16, 2 * depth), 1) % depth
    pick = ((row == 0) & (lane == 0)) | ((row == 1) & (lane == depth - 1))
    chosen = dot(pick.astype(F32).astype(BF16), both(plane, 1), ((1,), (1,)))
    return chosen[:2]


def rows_of(pieces, width):
    row = lax.broadcasted_iota(jnp.int32, (16, width), 0)
    value = jnp.zeros((16, width), F32)
    for number, piece in enumerate(pieces):
        value = jnp.where(row == number, piece.astype(F32), value)
    return value.astype(BF16)


def ends_kernel(rho_ref, ends_ref):
    ends_ref[0] = ends_of(rho_ref[0])


def height_kernel(planes, coupling, pivots, rho_ref, source_ref, halo_ref, x_ref, faces_ref):
    j = pl.program_id(0)
    rho = rho_ref[0]
    width, depth = rho.shape
    row = lax.broadcasted_iota(jnp.int32, rho.shape, 0)
    lane = lax.broadcasted_iota(jnp.int32, rho.shape, 1)
    below = jnp.where(row == 0, 0.0, pltpu.roll(rho, 1, 0))
    above = jnp.where(row == width - 1, 0.0, pltpu.roll(rho, width - 1, 0))
    before = jnp.where(lane == 0, 0.0, pltpu.roll(rho, 1, 1))
    after = jnp.where(lane == depth - 1, 0.0, pltpu.roll(rho, depth - 1, 1))
    left_high, left_low = split(halo_ref[0, 0:1])
    right_high, right_low = split(halo_ref[0, 1:2])
    first = (lax.broadcasted_iota(jnp.int32, (1, depth), 1) == 0).astype(F32)
    last = (lax.broadcasted_iota(jnp.int32, (1, depth), 1) == depth - 1).astype(F32)
    edge = dot(
        rows_of((left_high, left_low, right_high, right_low), width),
        rows_of((first, first, last, last), depth),
        ((0,), (0,)),
    )
    rhs = (
        2.0
        * (
            coupling[0] * (below + above - 2.0 * rho)
            + coupling[2] * (before + after + edge - 2.0 * rho)
        )
        + source_ref[0]
        + 2.0 * rho
    )
    strength = coupling[1]

    @pl.when(j == 0)
    def _():
        x_ref[0] = rhs * pivots[0]

    @pl.when(j > 0)
    def _():
        x_ref[j] = (rhs + strength * x_ref[jnp.maximum(j - 1, 0)]) * pivots[j]

    @pl.when(j == planes - 1)
    def _():
        shape = faces_ref.shape
        faces_ref[:, 0] = x_ref[planes - 1].reshape(shape[0], shape[2], shape[3])

        def back(step, unused):
            i = planes - 2 - step
            x_ref[i] = x_ref[i] + (strength * pivots[i]) * x_ref[i + 1]
            return unused

        lax.fori_loop(0, planes - 1, back, 0)
        faces_ref[:, 1] = x_ref[0].reshape(shape[0], shape[2], shape[3])


def lines_kernel(
    group, coupling, into, x_ref, rho_ref, faces_ref, width_ref, mixed_ref, depth_ref, z_ref, ends_ref
):
    j = pl.program_id(0)
    width, depth = x_ref.shape[1:]
    count, size = width_ref.shape[:2]
    enter = faces_ref[:, 0].reshape(width, depth)
    leave = faces_ref[:, 1].reshape(width, depth)
    rhs = jnp.concatenate(
        [
            x_ref[g]
            + into[0, j * group + g] * enter
            + into[1, j * group + g] * leave
            - 2.0 * rho_ref[g]
            for g in range(group)
        ],
        axis=1,
    )
    high, low = split(rhs)
    local, starts, stops = [], [], []
    for i in range(count):
        part = slice(i * size, (i + 1) * size)
        product = dot(mixed_ref[i], jnp.concatenate([high[part], low[part]], 0), ((1,), (0,)))
        local.append(product[:size] + product[size:])
        starts.append(coupling[0] * width_ref[i, :, 0:1])
        stops.append(coupling[0] * width_ref[i, :, size - 1 : size])
    carry = jnp.zeros((1, group * depth), F32)
    ahead, heads = [], []
    for i in range(count):
        ahead.append(carry)
        heads.append(local[i][0:1] + starts[i][0:1] * carry)
        carry = local[i][size - 1 :] + starts[i][size - 1 :] * carry
    carry = jnp.zeros((1, group * depth), F32)
    solved = [None] * count
    for i in reversed(range(count)):
        solved[i] = local[i] + starts[i] * ahead[i] + stops[i] * carry
        carry = heads[i] + stops[i][0:1] * carry
    solved = jnp.concatenate(solved, axis=0)
    for g in range(group):
        product = dot(both(solved[:, g * depth : (g + 1) * depth], 1), depth_ref[...], ((1,), (0,)))
        z = product[:, :depth] + product[:, depth:]
        z_ref[g] = z
        ends_ref[g] = ends_of(z)


def finish_kernel(group, rho_ref, z_ref, carry_ref, edge_ref, out_ref):
    width, depth = rho_ref.shape[1:]
    in_high, in_low = split(edge_ref[0:1])
    next_high, next_low = split(edge_ref[1:2])
    rhs = rows_of((in_high, in_high, in_low, next_high, next_high, next_low), depth)
    for g in range(group):
        a_high, a_low = split(carry_ref[g, 0:1])
        b_high, b_low = split(carry_ref[g, 1:2])
        lhs = rows_of((a_high, a_low, a_high, b_high, b_low, b_high), width)
        out_ref[g] = rho_ref[g] + z_ref[g] + dot(lhs, rhs, ((0,), (0,)))


def height_tables(strength, planes, count):
    root = (1.0 + 2.0 * strength + jnp.sqrt(1.0 + 4.0 * strength)) * 0.5
    ratio = strength / root
    log_ratio = jnp.log(ratio)

    def tail(index):
        return 1.0 - jnp.exp((2.0 * (index + 1.0)) * log_ratio)

    def power(index):
        return jnp.exp(index * log_ratio)

    base = (jnp.arange(count, dtype=F32) * planes)[:, None]
    j = jnp.arange(planes, dtype=F32)[None, :]
    pivots = tail(base + j) / (root * tail(base + j + 1.0))
    leave = power(planes - j) * tail(base + j) / tail(base + planes)
    base3, j3, m3 = base[:, :, None], j[:, :, None], j[:, None, :]
    distance = jnp.maximum(m3 - j3, 0.0)
    terms = (
        power(distance + m3 + 1.0)
        * (tail(base3 + j3) / tail(base3 + m3))
        * (tail(base3) / tail(base3 + m3 + 1.0))
    )
    enter = jnp.sum(jnp.where(m3 >= j3, terms, 0.0), axis=2)
    through = power(float(planes)) * tail(base[:, 0]) / tail(base[:, 0] + planes)
    return pivots, enter, leave, through


def per_device(density, source, coupling, width_inverse, height_inverse, depth_inverse):
    planes, width, depth = density.shape
    pencils, slabs = lax.axis_size("pencil"), lax.axis_size("slab")
    pencil, slab = lax.axis_index("pencil"), lax.axis_index("slab")
    size = depth_inverse.shape[1]
    group = 2
    smem = pl.BlockSpec(memory_space=pltpu.SMEM)
    params = pltpu.CompilerParams(
        dimension_semantics=("arbitrary",), vmem_limit_bytes=56 * 1024 * 1024
    )

    def whole(shape):
        return pl.BlockSpec(shape, lambda j: (0,) * len(shape))

    def per_plane(shape):
        return pl.BlockSpec(shape, lambda j: (j,) + (0,) * (len(shape) - 1))

    ends = pl.pallas_call(
        ends_kernel,
        grid=(planes,),
        out_shape=jax.ShapeDtypeStruct((planes, 2, width), F32),
        in_specs=[per_plane((1, width, depth))],
        out_specs=per_plane((1, 2, width)),
        compiler_params=params,
    )(density)
    up = [(i, i + 1) for i in range(slabs - 1)]
    down = [(i + 1, i) for i in range(slabs - 1)]
    left = lax.ppermute(ends[:, 1:2], "slab", up)
    right = lax.ppermute(ends[:, 0:1], "slab", down)
    halo = jnp.concatenate([left, right], axis=1)

    pivots, enter, leave, through = height_tables(coupling[1], planes, pencils)
    own_pivots = lax.dynamic_index_in_dim(pivots, pencil, 0, False)
    into = jnp.stack(
        [
            lax.dynamic_index_in_dim(enter, pencil, 0, False),
            lax.dynamic_index_in_dim(leave, pencil, 0, False),
        ]
    )
    share = width // pencils
    partial, faces = pl.pallas_call(
        lambda *refs: height_kernel(planes, *refs),
        grid=(planes,),
        out_shape=(
            jax.ShapeDtypeStruct((planes, width, depth), F32),
            jax.ShapeDtypeStruct((pencils, 2, share, depth), F32),
        ),
        in_specs=[
            smem,
            smem,
            per_plane((1, width, depth)),
            per_plane((1, width, depth)),
            per_plane((1, 2, width)),
        ],
        out_specs=(whole((planes, width, depth)), whole((pencils, 2, share, depth))),
        compiler_params=params,
    )(coupling, own_pivots, density, source, halo)

    held = lax.all_to_all(faces, "pencil", split_axis=0, concat_axis=0, tiled=True)
    entering = [jnp.zeros_like(held[0, 0])]
    for d in range(pencils - 1):
        entering.append(held[d, 0] + through[d] * entering[d])
    following = [None] * pencils
    following[pencils - 1] = jnp.zeros_like(held[0, 0])
    for d in range(pencils - 1, 0, -1):
        following[d - 1] = held[d, 1] + enter[d, 0] * entering[d] + leave[d, 0] * following[d]
    solved = jnp.stack([jnp.stack(pair) for pair in zip(entering, following)])
    solved = lax.all_to_all(solved, "pencil", split_axis=0, concat_axis=0, tiled=True)

    w_high, w_low = split_outside(width_inverse)
    mixed = jnp.concatenate(
        [
            jnp.concatenate([w_high, w_high], axis=2),
            jnp.concatenate([w_low, jnp.zeros_like(w_low)], axis=2),
        ],
        axis=1,
    )
    matrix = lax.dynamic_index_in_dim(depth_inverse, slab, 0, False).T
    d_high, d_low = split_outside(matrix)
    depth_mixed = jnp.concatenate(
        [
            jnp.concatenate([d_high, d_low], axis=1),
            jnp.concatenate([d_high, jnp.zeros_like(d_low)], axis=1),
        ],
        axis=0,
    )
    local, bounds = pl.pallas_call(
        lambda *refs: lines_kernel(group, *refs),
        grid=(planes // group,),
        out_shape=(
            jax.ShapeDtypeStruct((planes, width, depth), F32),
            jax.ShapeDtypeStruct((planes, 2, width), F32),
        ),
        in_specs=[
            smem,
            smem,
            per_plane((group, width, depth)),
            per_plane((group, width, depth)),
            whole(solved.shape),
            whole(width_inverse.shape),
            whole(mixed.shape),
            whole(depth_mixed.shape),
        ],
        out_specs=(per_plane((group, width, depth)), per_plane((group, 2, width))),
        compiler_params=params,
    )(coupling, into, partial, density, solved, width_inverse, mixed, depth_mixed)

    gathered = lax.all_gather(bounds, "slab")
    strength = coupling[2]
    zero = jnp.zeros((planes, width), F32)
    forward = [zero]
    for d in range(slabs - 1):
        forward.append(gathered[d, :, 1] + strength * depth_inverse[d, size - 1, 0] * forward[d])
    backward = [zero] * slabs
    for d in range(slabs - 1, 0, -1):
        backward[d - 1] = (
            gathered[d, :, 0]
            + strength * depth_inverse[d, 0, 0] * forward[d]
            + strength * depth_inverse[d, 0, size - 1] * backward[d]
        )
    carry_in, carry_next = forward[0], backward[0]
    for d in range(1, slabs):
        carry_in = jnp.where(slab == d, forward[d], carry_in)
        carry_next = jnp.where(slab == d, backward[d], carry_next)
    carries = jnp.stack([carry_in, carry_next], axis=1)
    edges = strength * jnp.stack([matrix[0], matrix[size - 1]])
    return pl.pallas_call(
        lambda *refs: finish_kernel(group, *refs),
        grid=(planes // group,),
        out_shape=jax.ShapeDtypeStruct((planes, width, depth), F32),
        in_specs=[
            per_plane((group, width, depth)),
            per_plane((group, width, depth)),
            per_plane((group, 2, width)),
            whole((2, depth)),
        ],
        out_specs=per_plane((group, width, depth)),
        compiler_params=params,
    )(density, local, carries, edges)


def solution(mesh):
    in_specs = (P("pencil", None, "slab"), P("pencil", None, "slab"), P(), P(), P(), P())
    out_specs = P("pencil", None, "slab")
    return jax.shard_map(
        per_device, mesh=mesh, in_specs=in_specs, out_specs=out_specs, check_vma=False
    )
```

time: 507 us -> 144 us (0.28)
  the two profiles are of different devices: /device:TPU:27 before, /device:TPU:0 now
where the time goes in v1:
time: 144 us; the launch traced here: 142 us
  Pallas kernels  54.3 us (38%)
  other arithmetic  22.4 us (16%)
  waiting for transfers between devices  20.6 us (14%)
  between operations  15.2 us (11%)
  starting transfers between devices  14.3 us (10%)
  local copies, waits for them, and re-layouts  8.74 us (6%)
  blocking collectives  6.35 us (4%)
    pallas_call x1, Pallas kernels, per_device(): pl.pallas_call(lambda *refs: height_kernel(planes, *refs), grid=(planes,)...  18.4 us
    all_to_all x1, waiting for transfers between devices, per_device(): lax.all_to_all(solved, 'pencil', split_axis=0, concat_axis=0, tiled=True)  17.1 us
    pallas_call x1, Pallas kernels, per_device(): pl.pallas_call(lambda *refs: lines_kernel(group, *refs), grid=(planes //...  14.2 us
    add x2, other arithmetic, per_device(): held[d, 1] + enter[d, 0] * entering[d] + leave[d, 0] * following[d]  12.6 us
    pallas_call x1, Pallas kernels, per_device(): pl.pallas_call(ends_kernel, grid=(planes,), out_shape=jax.ShapeDtypeStruc...  11.4 us
    pallas_call x1, Pallas kernels, per_device(): pl.pallas_call(lambda *refs: finish_kernel(group, *refs), grid=(planes //...  10.2 us
    all_gather x1, blocking collectives, per_device(): gathered = lax.all_gather(bounds, 'slab')  6.35 us
    all_to_all x1, starting transfers between devices, per_device(): lax.all_to_all(faces, 'pencil', split_axis=0, concat_axis=0, tiled=True)  6.1 us
  transfers between devices with their start and end apart: 4, of which 3 were waited for; matrix products, arithmetic and copies ran while one was open for 7% of the time, Pallas kernels for 0%

profile of v1, /device:TPU:0, one launch (start us, length us, event | category | flops | bytes accessed | tf_op | source)
XLA Modules:
  0.0 141.9 jit_solution(3732833027036059159)
XLA Ops:
  0.0 11.4 %shard_map.55 = f32[16,2,768]{2,1,0:T(2,128)} custom-call(f32[16,768,128]{2,1,0:T(8,128)} %refs_0_.5), custom_call_target="tpu_custom_call" | custom-call | tf_op jit(solution)/shard_map/pallas_call | solution.py:203
  11.4 1.1 fusion.57
  12.5 2.4 %collective-permute-start = (f32[16,1,768]{2,1,0:T(1,128)S(1)}, f32[16,1,768]{2,1,0:T(1,128)S(1)}, u32[]{:S(2)}, u32[]{:S(2)}) collective-permute-start(f32[16,1,768]{2,1,0:T(1,128)S(1)} %get-tuple-element.38), channel_id=1, source_target_pairs={{0,8},{8,16},{16,24},{1,9},{9,17},{17,25},{2,10},{10,18},{18,26},{... | collective-permute-start | bytes 147464 | tf_op jit(solution)/shard_map/ppermute | solution.py:213
  14.9 1.3 collective-permute-start.1
  16.2 0.7 fusion.61
  20.1 0.7 pad_maximum_fusion.refs_4_
  20.9 18.4 %shard_map.56 = (f32[16,768,128]{2,1,0:T(8,128)}, f32[8,2,96,128]{3,2,1,0:T(8,128)}) custom-call(f32[3]{0:T(128)} %refs_0_.4, f32[16]{0:T(128)} %fusion.43.refs_1_, f32[16,768,128]{2,1,0:T(8,128)} %refs_0_.5, f32[16,768,128]{2,1,0:T(8,128)} %refs_3_.2, f32[16,2,768]{2,1,0:T(2,128)} %pad_maximum_fusion.refs_4_), custom_call_target="tpu_custom_call" | custom-call | tf_op jit(solution)/shard_map/pallas_call | solution.py:226
  39.3 6.1 %all-to-all-start = ((f32[8,2,96,128]{3,2,1,0:T(8,128)}), f32[8,2,96,128]{3,2,1,0:T(8,128)S(1)}, u32[]{:S(2)}, u32[]{:S(2)}) async-start(f32[8,2,96,128]{3,2,1,0:T(8,128)} %get-tuple-element.10), calls=%async_computation | async-start | bytes 1572864 | tf_op jit(solution)/shard_map/all_to_all | solution.py:244
  45.4 1.5 %fusion.56 = (f32[1,1,1]{2,1,0:T(1,128)}, f32[1,1,1]{2,1,0:T(1,128)}, f32[1,1,1]{2,1,0:T(1,128)}, f32[1,1,1]{2,1,0:T(1,128)}, f32[1,1,1]{2,1,0:T(1,128)}, /*inde...) fusion(f32[4,128,128]{2,1,0:T(8,128)} %param.10), kind=kLoop, calls=%fused_computation.106 | loop fusion | bytes 72 | tf_op jit(solution)/shard_map/slice | solution.py:298
  58.6 0.9 constant_dynamic-slice_fusion
  59.6 0.7 fusion.62
  62.9 3.0 %all-to-all-done = f32[8,2,96,128]{3,2,1,0:T(8,128)S(1)} async-done(((f32[8,2,96,128]{3,2,1,0:T(8,128)}), f32[8,2,96,128]{3,2,1,0:T(8,128)S(1)}, u32[]{:S(2)}, u32[]{:S(2)}) %all-to-all-start) | async-done | bytes 786464 | tf_op jit(solution)/shard_map/all_to_all | solution.py:244
  65.9 4.4 %fusion.22 = (f32[1,96,128]{2,1,0:T(8,128)S(1)}, f32[1,96,128]{2,1,0:T(8,128)S(1)}, f32[1,96,128]{2,1,0:T(8,128)S(1)}, f32[1,96,128]{2,1,0:T(8,128)S(1)}, f32[1,...) fusion(f32[8,2,96,128]{3,2,1,0:T(8,128)S(1)} %all-to-all-done, ...), kind=kLoop, calls=%fused_computation.53 | loop fusion | flops 196608 | bytes 786468 | tf_op jit(solution)/shard_map/add | solution.py:251
  70.3 8.2 %fusion.40 = (f32[1,96,128]{2,1,0:T(8,128)S(1)}, f32[1,96,128]{2,1,0:T(8,128)S(1)}, f32[1,96,128]{2,1,0:T(8,128)S(1)}, f32[1,96,128]{2,1,0:T(8,128)S(1)}, f32[1,...) fusion(f32[8,2,96,128]{3,2,1,0:T(8,128)S(1)} %all-to-all-done, f32[1,96,128]{2,1,0:T(8,128)S(1)} %get-tuple-element.20, ...), kind=kLoop, calls=%fused_computation.83 | loop fusion | flops 331776 | bytes 983096 | tf_op jit(solution)/shard_map/add | solution.py:251
  78.5 0.6 bitcast_dynamic-update-slice_fusion.1
  79.2 0.7 fusion.5
  79.8 0.6 fusion.6
  80.5 0.6 fusion.7
  81.1 0.6 fusion.8
  81.8 0.6 fusion.9
  82.4 0.7 fusion.10
  83.1 0.6 bitcast_dynamic-update-slice_fusion
  83.7 4.5 %all-to-all-start.1 = ((f32[8,2,96,128]{3,2,1,0:T(8,128)}), f32[8,2,96,128]{3,2,1,0:T(8,128)S(1)}, u32[]{:S(2)}, u32[]{:S(2)}) async-start(f32[8,2,96,128]{3,2,1,0:T(8,128)} %bitcast_dynamic-update-slice_fusion), calls=%async_computation.1 | async-start | bytes 1572864 | tf_op jit(solution)/shard_map/all_to_all | solution.py:253
  88.8 1.3 maximum_multiply_fusion.refs_3_
  90.1 0.7 fusion.4.refs_7_
  90.9 1.0 fusion.1.refs_6_
  91.9 17.1 %all-to-all-done.1.refs_4_ = f32[8,2,96,128]{3,2,1,0:T(8,128)S(1)} async-done(((f32[8,2,96,128]{3,2,1,0:T(8,128)}), f32[8,2,96,128]{3,2,1,0:T(8,128)S(1)}, u32[]{:S(2)}, u32[]{:S(2)}) %all-to-all-start.1) | async-done | bytes 786464 | tf_op jit(solution)/shard_map/all_to_all | solution.py:253
  109.0 0.9 copy-done
  109.8 14.2 %shard_map.57 = (f32[16,768,128]{2,1,0:T(8,128)}, f32[16,2,768]{2,1,0:T(2,128)}) custom-call(f32[3]{0:T(128)} %refs_0_.4, f32[2,16]{1,0:T(2,128)} %pad_maximum_fusion.2.refs_1_, f32[16,768,128]{2,1,0:T(8,128)} %get-tuple-element.9.refs_2_, f32[16,768,128]{2,1,0:T(8,128)} %refs_0_.5, f32[8,2,96,128]{3,2,1,0:T(8,128)} %copy-done, f32[6,128,128]{2,1,0:T(8,128)} %refs_5_.1, ...), custom_call_target="tpu_custom_call" | custom-call | tf_op jit(solution)/shard_map/pallas_call | solution.py:272
  124.0 6.4 %all-gather = f32[64,2,768]{2,1,0:T(2,128)S(1)} all-gather(f32[16,2,768]{2,1,0:T(2,128)} %get-tuple-element.12), channel_id=2, replica_groups=mesh['slab'=4,'pencil'=8] {'slab'}, dimensions={0}, use_global_device_ids=true | all-gather | bytes 491520 | tf_op jit(solution)/shard_map/all_gather | solution.py:293
  130.9 0.7 pad_maximum_fusion.1.refs_2_
  131.6 10.2 %shard_map.58 = f32[16,768,128]{2,1,0:T(8,128)} custom-call(f32[16,768,128]{2,1,0:T(8,128)} %refs_0_.5, f32[16,768,128]{2,1,0:T(8,128)} %get-tuple-element.11.refs_1_, f32[16,2,768]{2,1,0:T(2,128)} %pad_maximum_fusion.1.refs_2_, f32[2,128]{1,0:T(2,128)} %maximum_multiply_fusion.refs_3_), custom_call_target="tpu_custom_call" | custom-call | tf_op jit(solution)/shard_map/pallas_call | solution.py:312
  (26 shorter events, 3.9 us)
Async XLA Ops:
  0.0 16.2 %copy-start.2 = (f32[3]{0:T(128)S(1)}, f32[3]{0:T(128)}, u32[]{:S(2)}) copy-start(f32[3]{0:T(128)} %refs_0_.4) | copy-start | bytes 40
  12.5 7.1 %collective-permute-start = (f32[16,1,768]{2,1,0:T(1,128)S(1)}, f32[16,1,768]{2,1,0:T(1,128)S(1)}, u32[]{:S(2)}, u32[]{:S(2)}) collective-permute-start(f32[16,1,768]{2,1,0:T(1,128)S(1)} %get-tuple-element.38), channel_id=1, source_target_pairs={{0,8},{8,16},{16,24},{1,9},{9,17},{17,25},{2,10},{10,18},{18,26},{... | collective-permute-start | bytes 147464 | tf_op jit(solution)/shard_map/ppermute | solution.py:213
  14.9 5.2 %collective-permute-start.1 = (f32[16,1,768]{2,1,0:T(1,128)S(1)}, f32[16,1,768]{2,1,0:T(1,128)S(1)}, u32[]{:S(2)}, u32[]{:S(2)}) collective-permute-start(f32[16,1,768]{2,1,0:T(1,128)S(1)} %get-tuple-element.39), channel_id=1, source_target_pairs={{8,0},{16,8},{24,16},{9,1},{17,9},{25,17},{10,2},{18,10},{26,18},{... | collective-permute-start | bytes 147464 | tf_op jit(solution)/shard_map/ppermute | solution.py:214
  39.3 26.6 %all-to-all-start = ((f32[8,2,96,128]{3,2,1,0:T(8,128)}), f32[8,2,96,128]{3,2,1,0:T(8,128)S(1)}, u32[]{:S(2)}, u32[]{:S(2)}) async-start(f32[8,2,96,128]{3,2,1,0:T(8,128)} %get-tuple-element.10), calls=%async_computation | async-start | bytes 1572864 | tf_op jit(solution)/shard_map/all_to_all | solution.py:244
  79.8 11.0 %copy-start.1 = (f32[6,128,128]{2,1,0:T(8,128)S(1)}, f32[6,128,128]{2,1,0:T(8,128)}, u32[]{:S(2)}) copy-start(f32[6,128,128]{2,1,0:T(8,128)} %refs_5_.1) | copy-start | bytes 1179652
  83.7 25.3 %all-to-all-start.1 = ((f32[8,2,96,128]{3,2,1,0:T(8,128)}), f32[8,2,96,128]{3,2,1,0:T(8,128)S(1)}, u32[]{:S(2)}, u32[]{:S(2)}) async-start(f32[8,2,96,128]{3,2,1,0:T(8,128)} %bitcast_dynamic-update-slice_fusion), calls=%async_computation.1 | async-start | bytes 1572864 | tf_op jit(solution)/shard_map/all_to_all | solution.py:253
  108.9 0.9 copy-start

commit v2 on v1

v2 whole, which is shorter than its diff:
```python
import jax
import jax.numpy as jnp
from jax import lax
from jax.experimental import pallas as pl
from jax.experimental.pallas import tpu as pltpu
from jax.sharding import PartitionSpec as P

F32, BF16 = jnp.float32, jnp.bfloat16
MESH = pl.DeviceIdType.MESH


def split(value):
    high = value.astype(BF16)
    return high, (value - high.astype(F32)).astype(BF16)


def split_outside(value):
    high = lax.reduce_precision(value, 8, 7)
    return high.astype(BF16), (value - high).astype(BF16)


def both(value, axis):
    return jnp.concatenate(split(value), axis=axis)


def dot(a, b, dims):
    return lax.dot_general(a, b, (dims, ((), ())), preferred_element_type=F32)


def ends_of(plane):
    width, depth = plane.shape
    row = lax.broadcasted_iota(jnp.int32, (depth, depth), 0)
    lane = lax.broadcasted_iota(jnp.int32, (depth, depth), 1)
    lines = []
    for column in (0, depth - 1):
        pieces = []
        for start in range(0, width, depth):
            edge = plane[start : start + depth, column : column + 1]
            pieces.append(jnp.sum(jnp.where(row == lane, edge, 0.0), axis=0, keepdims=True))
        lines.append(jnp.concatenate(pieces, axis=1))
    return jnp.concatenate(lines, axis=0)


def rows_of(pieces, width):
    row = lax.broadcasted_iota(jnp.int32, (16, width), 0)
    value = jnp.zeros((16, width), F32)
    for number, piece in enumerate(pieces):
        value = jnp.where(row == number, piece.astype(F32), value)
    return value.astype(BF16)


def ends_kernel(slabs, group, rho_ref, halo_ref, ends_ref, got_ref, send_sem, recv_sem):
    j = pl.program_id(0)
    me = lax.axis_index("slab")
    nxt, prv = lax.rem(me + 1, slabs), lax.rem(me + slabs - 1, slabs)
    barrier = pltpu.get_barrier_semaphore()

    @pl.when(j == 0)
    def _():
        for peer in (nxt, prv):
            pl.semaphore_signal(barrier, inc=1, device_id={"slab": peer}, device_id_type=MESH)
        pl.semaphore_wait(barrier, 2)

    for g in range(group):
        pair = ends_of(rho_ref[g])
        ends_ref[0, j * group + g] = pair[0:1]
        ends_ref[1, j * group + g] = pair[1:2]

    @pl.when(j == pl.num_programs(0) - 1)
    def _():
        copies = [
            pltpu.make_async_remote_copy(
                src_ref=ends_ref.at[1 - way],
                dst_ref=got_ref.at[way],
                send_sem=send_sem.at[way],
                recv_sem=recv_sem.at[way],
                device_id={"slab": peer},
                device_id_type=MESH,
            )
            for way, peer in ((0, nxt), (1, prv))
        ]
        for copy in copies:
            copy.start()
        for copy in copies:
            copy.wait()
        halo_ref[0] = jnp.where(me == 0, 0.0, got_ref[0])
        halo_ref[1] = jnp.where(me == slabs - 1, 0.0, got_ref[1])


def height_kernel(
    planes, group, coupling, pivots, rho_ref, source_ref, halo_ref, x_ref, faces_ref, kept_ref
):
    step = pl.program_id(0)
    width, depth = rho_ref.shape[1:]
    strength = coupling[1]
    row = lax.broadcasted_iota(jnp.int32, (width, depth), 0)
    lane = lax.broadcasted_iota(jnp.int32, (width, depth), 1)
    first = (lax.broadcasted_iota(jnp.int32, (1, depth), 1) == 0).astype(F32)
    last = (lax.broadcasted_iota(jnp.int32, (1, depth), 1) == depth - 1).astype(F32)
    units = rows_of((first, first, last, last), depth)

    @pl.when(step == 0)
    def _():
        x_ref[planes - 1] = jnp.zeros((width, depth), F32)

    for g in range(group):
        j = step * group + g
        rho = rho_ref[g]
        below = jnp.where(row == 0, 0.0, pltpu.roll(rho, 1, 0))
        above = jnp.where(row == width - 1, 0.0, pltpu.roll(rho, width - 1, 0))
        before = jnp.where(lane == 0, 0.0, pltpu.roll(rho, 1, 1))
        after = jnp.where(lane == depth - 1, 0.0, pltpu.roll(rho, depth - 1, 1))
        left_high, left_low = split(halo_ref[0, g])
        right_high, right_low = split(halo_ref[1, g])
        edge = dot(rows_of((left_high, left_low, right_high, right_low), width), units, ((0,), (0,)))
        rhs = (
            2.0
            * (
                coupling[0] * (below + above - 2.0 * rho)
                + coupling[2] * (before + after + edge - 2.0 * rho)
            )
            + source_ref[g]
            + 2.0 * rho
        )
        kept_ref[j] = 2.0 * rho
        x_ref[j] = (rhs + strength * x_ref[lax.rem(j + planes - 1, planes)]) * pivots[j]

    @pl.when(step == planes // group - 1)
    def _():
        shape = faces_ref.shape
        faces_ref[:, 0] = x_ref[planes - 1].reshape(shape[0], shape[2], shape[3])

        def back(count, unused):
            i = planes - 2 - count
            later = x_ref[i + 1]
            x_ref[i] = x_ref[i] + (strength * pivots[i]) * later
            x_ref[i + 1] = later - kept_ref[i + 1]
            return unused

        lax.fori_loop(0, planes - 1, back, 0)
        faces_ref[:, 1] = x_ref[0].reshape(shape[0], shape[2], shape[3])
        x_ref[0] = x_ref[0] - kept_ref[0]


def solve_group(rhs, strength, width_ref, mixed_ref, depth_mixed):
    count, size = width_ref.shape[:2]
    depth = size
    total = rhs.shape[1]
    high, low = split(rhs)
    local, starts, stops = [], [], []
    for i in range(count):
        part = slice(i * size, (i + 1) * size)
        product = dot(mixed_ref[i], jnp.concatenate([high[part], low[part]], 0), ((1,), (0,)))
        local.append(product[:size] + product[size:])
        starts.append(strength * width_ref[i, :, 0:1])
        stops.append(strength * width_ref[i, :, size - 1 : size])
    carry = jnp.zeros((1, total), F32)
    ahead, heads = [], []
    for i in range(count):
        ahead.append(carry)
        heads.append(local[i][0:1] + starts[i][0:1] * carry)
        carry = local[i][size - 1 :] + starts[i][size - 1 :] * carry
    carry = jnp.zeros((1, total), F32)
    solved = [None] * count
    for i in reversed(range(count)):
        solved[i] = local[i] + starts[i] * ahead[i] + stops[i] * carry
        carry = heads[i] + stops[i][0:1] * carry
    solved = jnp.concatenate(solved, axis=0)
    answers = []
    for start in range(0, total, depth):
        product = dot(both(solved[:, start : start + depth], 1), depth_mixed, ((1,), (0,)))
        answers.append(product[:, :depth] + product[:, depth:])
    return answers


def lines_kernel(
    group, pencils, slabs,
    coupling, into, chain, links,
    u_ref, faces_ref, width_ref, mixed_ref, depth_ref,
    z_ref, carry_ref,
    held, solved, final, face_z, ends, gathered,
    send_one, recv_one, send_two, recv_two, send_three, recv_three,
):
    planes, width, depth = u_ref.shape
    me, slab = lax.axis_index("pencil"), lax.axis_index("slab")
    barrier = pltpu.get_barrier_semaphore()
    for k in range(1, pencils):
        pl.semaphore_signal(
            barrier, inc=1, device_id={"pencil": lax.rem(me + k, pencils)}, device_id_type=MESH
        )
    for k in range(1, slabs):
        pl.semaphore_signal(
            barrier, inc=1, device_id={"slab": lax.rem(slab + k, slabs)}, device_id_type=MESH
        )
    pl.semaphore_wait(barrier, pencils + slabs - 2)

    def exchange(source, target, send, recv):
        copies = []
        for k in range(1, pencils):
            peer = lax.rem(me + k, pencils)
            copy = pltpu.make_async_remote_copy(
                src_ref=source.at[peer],
                dst_ref=target.at[me],
                send_sem=send.at[k - 1],
                recv_sem=recv.at[k - 1],
                device_id={"pencil": peer},
                device_id_type=MESH,
            )
            copy.start()
            copies.append(copy)
        target[me] = source[me]
        return copies

    def some(begin, end):
        def body(index, unused):
            base = index * group
            rhs = jnp.concatenate([u_ref[base + g] for g in range(group)], axis=1)
            answers = solve_group(rhs, coupling[0], width_ref, mixed_ref, depth_ref[...])
            for g in range(group):
                z_ref[base + g] = answers[g]
            return unused

        lax.fori_loop(begin, end, body, 0)

    groups = planes // group
    copies = exchange(faces_ref, held, send_one, recv_one)
    some(0, groups // 2)
    for copy in copies:
        copy.wait()
    value = jnp.zeros(held.shape[2:], F32)
    for d in range(pencils):
        solved[d, 0] = value
        if d < pencils - 1:
            value = held[d, 0] + chain[0, d] * value
    value = jnp.zeros(held.shape[2:], F32)
    for d in reversed(range(pencils)):
        solved[d, 1] = value
        if d > 0:
            value = held[d, 1] + chain[1, d] * solved[d, 0] + chain[2, d] * value
    copies = exchange(solved, final, send_two, recv_two)
    some(groups // 2, groups)
    for copy in copies:
        copy.wait()
    rhs = jnp.concatenate([final[:, side].reshape(width, depth) for side in range(2)], axis=1)
    answers = solve_group(rhs, coupling[0], width_ref, mixed_ref, depth_ref[...])
    for side in range(2):
        face_z[side] = answers[side]

    def correct(j, unused):
        z = z_ref[j] + into[0, j] * face_z[0] + into[1, j] * face_z[1]
        z_ref[j] = z
        ends[j] = ends_of(z)
        return unused

    lax.fori_loop(0, planes, correct, 0)
    copies = []
    for k in range(1, slabs):
        copy = pltpu.make_async_remote_copy(
            src_ref=ends,
            dst_ref=gathered.at[slab],
            send_sem=send_three.at[k - 1],
            recv_sem=recv_three.at[k - 1],
            device_id={"slab": lax.rem(slab + k, slabs)},
            device_id_type=MESH,
        )
        copy.start()
        copies.append(copy)
    gathered[slab] = ends[...]
    for copy in copies:
        copy.wait()
    zero = jnp.zeros((planes, width), F32)
    forward = [zero]
    for d in range(slabs - 1):
        forward.append(gathered[d, :, 1] + links[0, d] * forward[d])
    backward = [zero] * slabs
    for d in range(slabs - 1, 0, -1):
        backward[d - 1] = (
            gathered[d, :, 0] + links[1, d] * forward[d] + links[2, d] * backward[d]
        )
    carry_in, carry_next = forward[0], backward[0]
    for d in range(1, slabs):
        carry_in = jnp.where(slab == d, forward[d], carry_in)
        carry_next = jnp.where(slab == d, backward[d], carry_next)
    carry_ref[:, 0] = carry_in
    carry_ref[:, 1] = carry_next


def finish_kernel(group, rho_ref, z_ref, carry_ref, edge_ref, out_ref):
    width, depth = rho_ref.shape[1:]
    in_high, in_low = split(edge_ref[0:1])
    next_high, next_low = split(edge_ref[1:2])
    rhs = rows_of((in_high, in_high, in_low, next_high, next_high, next_low), depth)
    for g in range(group):
        a_high, a_low = split(carry_ref[g, 0:1])
        b_high, b_low = split(carry_ref[g, 1:2])
        lhs = rows_of((a_high, a_low, a_high, b_high, b_low, b_high), width)
        out_ref[g] = rho_ref[g] + z_ref[g] + dot(lhs, rhs, ((0,), (0,)))


def height_tables(strength, planes, count):
    root = (1.0 + 2.0 * strength + jnp.sqrt(1.0 + 4.0 * strength)) * 0.5
    ratio = strength / root
    log_ratio = jnp.log(ratio)

    def tail(index):
        return 1.0 - jnp.exp((2.0 * (index + 1.0)) * log_ratio)

    def power(index):
        return jnp.exp(index * log_ratio)

    base = (jnp.arange(count, dtype=F32) * planes)[:, None]
    j = jnp.arange(planes, dtype=F32)[None, :]
    pivots = tail(base + j) / (root * tail(base + j + 1.0))
    leave = power(planes - j) * tail(base + j) / tail(base + planes)
    base3, j3, m3 = base[:, :, None], j[:, :, None], j[:, None, :]
    distance = jnp.maximum(m3 - j3, 0.0)
    terms = (
        power(distance + m3 + 1.0)
        * (tail(base3 + j3) / tail(base3 + m3))
        * (tail(base3) / tail(base3 + m3 + 1.0))
    )
    enter = jnp.sum(jnp.where(m3 >= j3, terms, 0.0), axis=2)
    through = power(float(planes)) * tail(base[:, 0]) / tail(base[:, 0] + planes)
    return pivots, enter, leave, through


def per_device(density, source, coupling, width_inverse, height_inverse, depth_inverse):
    planes, width, depth = density.shape
    pencils, slabs = lax.axis_size("pencil"), lax.axis_size("slab")
    pencil, slab = lax.axis_index("pencil"), lax.axis_index("slab")
    size = depth_inverse.shape[1]
    group = 2
    smem = pl.BlockSpec(memory_space=pltpu.SMEM)
    params = pltpu.CompilerParams(
        dimension_semantics=("arbitrary",), vmem_limit_bytes=56 * 1024 * 1024
    )

    def whole(shape):
        return pl.BlockSpec(shape, lambda j: (0,) * len(shape))

    def per_plane(shape):
        return pl.BlockSpec(shape, lambda j: (j,) + (0,) * (len(shape) - 1))

    def plane_pairs(shape):
        return pl.BlockSpec(shape, lambda j: (0, j, 0, 0))

    vmem = pl.BlockSpec(memory_space=pltpu.VMEM)
    dma = pltpu.SemaphoreType.DMA
    strip = (2, planes, 1, width)
    halo = pl.pallas_call(
        lambda *refs: ends_kernel(slabs, 4, *refs),
        grid=(planes // 4,),
        out_shape=jax.ShapeDtypeStruct(strip, F32),
        in_specs=[per_plane((4, width, depth))],
        out_specs=whole(strip),
        scratch_shapes=[pltpu.VMEM(strip, F32), pltpu.VMEM(strip, F32), dma((2,)), dma((2,))],
        compiler_params=pltpu.CompilerParams(
            dimension_semantics=("arbitrary",),
            vmem_limit_bytes=56 * 1024 * 1024,
            collective_id=0,
            has_side_effects=True,
        ),
    )(density)

    pivots, enter, leave, through = height_tables(coupling[1], planes, pencils)
    own_pivots = lax.dynamic_index_in_dim(pivots, pencil, 0, False)
    into = jnp.stack(
        [
            lax.dynamic_index_in_dim(enter, pencil, 0, False),
            lax.dynamic_index_in_dim(leave, pencil, 0, False),
        ]
    )
    share = width // pencils
    partial, faces = pl.pallas_call(
        lambda *refs: height_kernel(planes, group, *refs),
        grid=(planes // group,),
        out_shape=(
            jax.ShapeDtypeStruct((planes, width, depth), F32),
            jax.ShapeDtypeStruct((pencils, 2, share, depth), F32),
        ),
        in_specs=[
            smem,
            smem,
            per_plane((group, width, depth)),
            per_plane((group, width, depth)),
            plane_pairs((2, group, 1, width)),
        ],
        out_specs=(whole((planes, width, depth)), whole((pencils, 2, share, depth))),
        scratch_shapes=[pltpu.VMEM((planes, width, depth), F32)],
        compiler_params=params,
    )(coupling, own_pivots, density, source, halo)

    w_high, w_low = split_outside(width_inverse)
    mixed = jnp.concatenate(
        [
            jnp.concatenate([w_high, w_high], axis=2),
            jnp.concatenate([w_low, jnp.zeros_like(w_low)], axis=2),
        ],
        axis=1,
    )
    matrix = lax.dynamic_index_in_dim(depth_inverse, slab, 0, False).T
    d_high, d_low = split_outside(matrix)
    depth_mixed = jnp.concatenate(
        [
            jnp.concatenate([d_high, d_low], axis=1),
            jnp.concatenate([d_high, jnp.zeros_like(d_low)], axis=1),
        ],
        axis=0,
    )
    strength = coupling[2]
    chain = jnp.stack([through, enter[:, 0], leave[:, 0]])
    links = strength * jnp.stack(
        [depth_inverse[:, size - 1, 0], depth_inverse[:, 0, 0], depth_inverse[:, 0, size - 1]]
    )
    pieces = pltpu.VMEM((pencils, 2, share, depth), F32)
    local, carries = pl.pallas_call(
        lambda *refs: lines_kernel(group, pencils, slabs, *refs),
        out_shape=(
            jax.ShapeDtypeStruct((planes, width, depth), F32),
            jax.ShapeDtypeStruct((planes, 2, width), F32),
        ),
        in_specs=[smem] * 4 + [vmem] * 5,
        out_specs=(vmem, vmem),
        scratch_shapes=[
            pieces,
            pieces,
            pieces,
            pltpu.VMEM((2, width, depth), F32),
            pltpu.VMEM((planes, 2, width), F32),
            pltpu.VMEM((slabs, planes, 2, width), F32),
            dma((pencils - 1,)),
            dma((pencils - 1,)),
            dma((pencils - 1,)),
            dma((pencils - 1,)),
            dma((slabs - 1,)),
            dma((slabs - 1,)),
        ],
        compiler_params=pltpu.CompilerParams(
            vmem_limit_bytes=56 * 1024 * 1024, collective_id=1, has_side_effects=True
        ),
    )(coupling, into, chain, links, partial, faces, width_inverse, mixed, depth_mixed)

    edges = strength * jnp.stack([matrix[0], matrix[size - 1]])
    return pl.pallas_call(
        lambda *refs: finish_kernel(group, *refs),
        grid=(planes // group,),
        out_shape=jax.ShapeDtypeStruct((planes, width, depth), F32),
        in_specs=[
            per_plane((group, width, depth)),
            per_plane((group, width, depth)),
            per_plane((group, 2, width)),
            whole((2, depth)),
        ],
        out_specs=per_plane((group, width, depth)),
        compiler_params=params,
    )(density, local, carries, edges)


def solution(mesh):
    in_specs = (P("pencil", None, "slab"), P("pencil", None, "slab"), P(), P(), P(), P())
    out_specs = P("pencil", None, "slab")
    return jax.shard_map(
        per_device, mesh=mesh, in_specs=in_specs, out_specs=out_specs, check_vma=False
    )
```

time: 144 us -> 106 us (0.74)
  the two profiles are of different devices: /device:TPU:0 before, /device:TPU:27 now
where the time goes in v2:
time: 106 us
  Pallas kernels  93.7 us (88%)
  other arithmetic  5.66 us (5%)
  local copies, waits for them, and re-layouts  4.07 us (4%)
  between operations  2.32 us (2%)
    pallas_call x1, Pallas kernels, per_device(): pl.pallas_call(lambda *refs: lines_kernel(group, pencils, slabs, *refs),...  57.8 us
    pallas_call x1, Pallas kernels, per_device(): pl.pallas_call(lambda *refs: height_kernel(planes, group, *refs), grid=(p...  15 us
    pallas_call x1, Pallas kernels, per_device(): pl.pallas_call(lambda *refs: ends_kernel(slabs, 4, *refs), grid=(planes /...  10.6 us
    pallas_call x1, Pallas kernels, per_device(): pl.pallas_call(lambda *refs: finish_kernel(group, *refs), grid=(planes //...  10.3 us

profile of v2, /device:TPU:27, one launch (start us, length us, event | category | flops | bytes accessed | tf_op | source)
XLA Modules:
  0.0 105.8 jit_solution(16186521437649733608)
XLA Ops:
  0.0 1.4 %fusion.12 = (f32[1]{0:T(128)}, f32[1]{0:T(128)}) fusion(f32[3]{0:T(128)} %refs_0_.6), kind=kLoop, calls=%fused_computation.44 | loop fusion | bytes 16 | tf_op jit(solution)/shard_map/slice | solution.py:410
  3.7 1.0 slice_reduce_fusion.4
  4.7 1.2 %maximum_multiply_fusion.refs_3_ = f32[3,4]{1,0:T(4,128)} fusion(f32[1,4]{1,0:T(1,128)S(1)} %bitcast.19, f32[1,4]{1,0:T(1,128)S(1)} %bitcast.18, f32[1,4]{1,0:T(1,128)S(1)} %bitcast.17, f32[]{:T(128)} %bitcast.1), kind=kLoop, calls=%fused_computation.27 | loop fusion | flops 36 | bytes 100 | tf_op jit(solution)/shard_map/mul | solution.py:412
  6.0 0.1 multiply_divide_fusion
  6.0 0.2 fusion.7
  6.2 0.5 fusion.10.refs_1_
  6.7 0.1 slice_reduce_fusion.1
  6.8 0.1 slice_reduce_fusion
  7.0 0.6 pad_maximum_fusion.1.refs_1_
  7.6 0.6 pad_maximum_fusion.refs_2_
  8.1 0.8 constant_dynamic-slice_fusion
  9.0 0.1 copy.8
  9.1 1.2 %maximum_multiply_fusion.1.refs_3_ = f32[2,128]{1,0:T(2,128)} fusion(f32[1,128]{1,0:T(1,128)S(1)} %get-tuple-element.19, f32[1,128]{1,0:T(1,128)S(1)} %get-tuple-element.18, f32[]{:T(128)} %bitcast.1), kind=kLoop, calls=%fused_computation.32 | loop fusion | flops 512 | bytes 2052 | tf_op jit(solution)/shard_map/mul | solution.py:443
  10.3 0.7 fusion.4.refs_8_
  11.0 0.0 copy-start
  11.0 10.6 %shard_map.55.refs_4_ = f32[2,16,1,768]{3,2,1,0:T(1,128)} custom-call(f32[16,768,128]{2,1,0:T(8,128)} %refs_0_.7), custom_call_target="tpu_custom_call" | custom-call | tf_op jit(solution)/shard_map/pallas_call | solution.py:350
  21.6 0.0 copy-done
  21.6 0.1 reduce-precision_convert_fusion
  21.7 0.9 fusion.1.refs_7_
  22.7 15.0 %shard_map.56 = (f32[16,768,128]{2,1,0:T(8,128)}, f32[8,2,96,128]{3,2,1,0:T(8,128)}) custom-call(f32[3]{0:T(128)} %refs_0_.6, f32[16]{0:T(128)} %fusion.10.refs_1_, f32[16,768,128]{2,1,0:T(8,128)} %refs_0_.7, f32[16,768,128]{2,1,0:T(8,128)} %refs_3_.1, f32[2,16,1,768]{3,2,1,0:T(1,128)} %shard_map.55.refs_4_), custom_call_target="tpu_custom_call" | custom-call | tf_op jit(solution)/shard_map/pallas_call | solution.py:374
  37.7 57.8 %shard_map.57 = (f32[16,768,128]{2,1,0:T(8,128)}, f32[16,2,768]{2,1,0:T(2,128)}) custom-call(f32[3]{0:T(128)} %refs_0_.6, f32[2,16]{1,0:T(2,128)} %pad_maximum_fusion.1.refs_1_, f32[3,8]{1,0:T(4,128)} %pad_maximum_fusion.refs_2_, f32[3,4]{1,0:T(4,128)} %maximum_multiply_fusion.refs_3_, f32[16,768,128]{2,1,0:T(8,128)} %get-tuple-element.9.refs_4_, ...), custom_call_target="tpu_custom_call" | custom-call | tf_op jit(solution)/shard_map/pallas_call | solution.py:416
  95.5 10.3 %shard_map.58 = f32[16,768,128]{2,1,0:T(8,128)} custom-call(f32[16,768,128]{2,1,0:T(8,128)} %refs_0_.7, f32[16,768,128]{2,1,0:T(8,128)} %get-tuple-element.11.refs_1_, f32[16,2,768]{2,1,0:T(2,128)} %get-tuple-element.12.refs_2_, f32[2,128]{1,0:T(2,128)} %maximum_multiply_fusion.1.refs_3_), custom_call_target="tpu_custom_call" | custom-call | tf_op jit(solution)/shard_map/pallas_call | solution.py:444
  (10 shorter events, 0.1 us)
Async XLA Ops:
  11.0 10.7 %copy-start = (f32[6,128,128]{2,1,0:T(8,128)S(1)}, f32[6,128,128]{2,1,0:T(8,128)}, u32[]{:S(2)}) copy-start(f32[6,128,128]{2,1,0:T(8,128)} %refs_6_.1) | copy-start | bytes 1179652

commit v3 on v2

--- a/solution.py
+++ b/solution.py
@@ -12,11 +12,6 @@
 def split(value):
     high = value.astype(BF16)
     return high, (value - high.astype(F32)).astype(BF16)
-
-
-def split_outside(value):
-    high = lax.reduce_precision(value, 8, 7)
-    return high.astype(BF16), (value - high).astype(BF16)
 
 
 def both(value, axis):
@@ -49,6 +44,38 @@
     return value.astype(BF16)
 
 
+class Heights:
+    def __init__(self, strength, planes, lanes):
+        self.shape, self.planes = (1, lanes), planes
+        strength = jnp.full(self.shape, strength, F32)
+        self.root = (1.0 + 2.0 * strength + jnp.sqrt(1.0 + 4.0 * strength)) * 0.5
+        self.log_ratio = jnp.log(strength / self.root)
+
+    def power(self, index):
+        return jnp.exp(jnp.full(self.shape, index, jnp.int32).astype(F32) * self.log_ratio)
+
+    def tail(self, index):
+        return 1.0 - self.power(2 * (index + 1))
+
+    def pivot(self, index):
+        return self.tail(index) / (self.root * self.tail(index + 1))
+
+    def enter(self, device, j):
+        base = device * self.planes
+        return (
+            self.power(j + 1)
+            * (self.tail(base) / self.tail(base + self.planes))
+            * (self.tail(self.planes - j - 1) / self.tail(0))
+        )
+
+    def leave(self, device, j):
+        base = device * self.planes
+        return self.power(self.planes - j) * (self.tail(base + j) / self.tail(base + self.planes))
+
+    def through(self, device):
+        return self.enter(device, self.planes - 1)
+
+
 def ends_kernel(slabs, group, rho_ref, halo_ref, ends_ref, got_ref, send_sem, recv_sem):
     j = pl.program_id(0)
     me = lax.axis_index("slab")
@@ -59,7 +86,6 @@
     def _():
         for peer in (nxt, prv):
             pl.semaphore_signal(barrier, inc=1, device_id={"slab": peer}, device_id_type=MESH)
-        pl.semaphore_wait(barrier, 2)
 
     for g in range(group):
         pair = ends_of(rho_ref[g])
@@ -68,6 +94,7 @@
 
     @pl.when(j == pl.num_programs(0) - 1)
     def _():
+        pl.semaphore_wait(barrier, 2)
         copies = [
             pltpu.make_async_remote_copy(
                 src_ref=ends_ref.at[1 - way],
@@ -88,7 +115,7 @@
 
 
 def height_kernel(
-    planes, group, coupling, pivots, rho_ref, source_ref, halo_ref, x_ref, faces_ref, kept_ref
+    planes, group, coupling, rho_ref, source_ref, halo_ref, x_ref, faces_ref, kept_ref
 ):
     step = pl.program_id(0)
     width, depth = rho_ref.shape[1:]
@@ -98,6 +125,8 @@
     first = (lax.broadcasted_iota(jnp.int32, (1, depth), 1) == 0).astype(F32)
     last = (lax.broadcasted_iota(jnp.int32, (1, depth), 1) == depth - 1).astype(F32)
     units = rows_of((first, first, last, last), depth)
+    heights = Heights(strength, planes, depth)
+    base = lax.axis_index("pencil") * planes
 
     @pl.when(step == 0)
     def _():
@@ -123,7 +152,7 @@
             + 2.0 * rho
         )
         kept_ref[j] = 2.0 * rho
-        x_ref[j] = (rhs + strength * x_ref[lax.rem(j + planes - 1, planes)]) * pivots[j]
+        x_ref[j] = (rhs + strength * x_ref[lax.rem(j + planes - 1, planes)]) * heights.pivot(base + j)
 
     @pl.when(step == planes // group - 1)
     def _():
@@ -133,7 +162,7 @@
         def back(count, unused):
             i = planes - 2 - count
             later = x_ref[i + 1]
-            x_ref[i] = x_ref[i] + (strength * pivots[i]) * later
+            x_ref[i] = x_ref[i] + (strength * heights.pivot(base + i)) * later
             x_ref[i + 1] = later - kept_ref[i + 1]
             return unused
 
@@ -175,13 +204,16 @@
 
 def lines_kernel(
     group, pencils, slabs,
-    coupling, into, chain, links,
-    u_ref, faces_ref, width_ref, mixed_ref, depth_ref,
-    z_ref, carry_ref,
+    coupling,
+    u_hbm, faces_ref, width_ref, depth_ref,
+    z_hbm, carry_ref,
+    u_ref, z_ref, mixed_ref, mixed_depth,
     held, solved, final, face_z, ends, gathered,
-    send_one, recv_one, send_two, recv_two, send_three, recv_three,
+    send_one, recv_one, send_two, recv_two, send_three, recv_three, load_sem, store_sem,
 ):
     planes, width, depth = u_ref.shape
+    groups = planes // group
+    count, size = width_ref.shape[:2]
     me, slab = lax.axis_index("pencil"), lax.axis_index("slab")
     barrier = pltpu.get_barrier_semaphore()
     for k in range(1, pencils):
@@ -192,7 +224,29 @@
         pl.semaphore_signal(
             barrier, inc=1, device_id={"slab": lax.rem(slab + k, slabs)}, device_id_type=MESH
         )
+
+    def load(index):
+        part = pl.ds(index * group, group)
+        return pltpu.make_async_copy(u_hbm.at[part], u_ref.at[part], load_sem.at[index])
+
+    def store(j):
+        return pltpu.make_async_copy(z_ref.at[j], z_hbm.at[j], store_sem.at[j])
+
+    for index in range(groups):
+        load(index).start()
+    for i in range(count):
+        high, low = split(width_ref[i])
+        mixed_ref[i, :size, :size] = high
+        mixed_ref[i, :size, size:] = high
+        mixed_ref[i, size:, :size] = low
+        mixed_ref[i, size:, size:] = jnp.zeros_like(low)
+    high, low = split(depth_ref[slab])
+    mixed_depth[:size, :size] = high
+    mixed_depth[size:, :size] = high
+    mixed_depth[:size, size:] = low
+    mixed_depth[size:, size:] = jnp.zeros_like(low)
     pl.semaphore_wait(barrier, pencils + slabs - 2)
+    heights = Heights(coupling[1], planes, depth)
 
     def exchange(source, target, send, recv):
         copies = []
@@ -214,15 +268,16 @@
     def some(begin, end):
         def body(index, unused):
             base = index * group
+            load(index).wait()
             rhs = jnp.concatenate([u_ref[base + g] for g in range(group)], axis=1)
-            answers = solve_group(rhs, coupling[0], width_ref, mixed_ref, depth_ref[...])
+            answers = solve_group(rhs, coupling[0], width_ref, mixed_ref, mixed_depth[...])
             for g in range(group):
                 z_ref[base + g] = answers[g]
+                ends[base + g] = ends_of(answers[g])
             return unused
 
         lax.fori_loop(begin, end, body, 0)
 
-    groups = planes // group
     copies = exchange(faces_ref, held, send_one, recv_one)
     some(0, groups // 2)
     for copy in copies:
@@ -231,28 +286,38 @@
     for d in range(pencils):
         solved[d, 0] = value
         if d < pencils - 1:
-            value = held[d, 0] + chain[0, d] * value
+            value = held[d, 0] + heights.through(d) * value
     value = jnp.zeros(held.shape[2:], F32)
     for d in reversed(range(pencils)):
         solved[d, 1] = value
         if d > 0:
-            value = held[d, 1] + chain[1, d] * solved[d, 0] + chain[2, d] * value
+            value = held[d, 1] + heights.enter(d, 0) * solved[d, 0] + heights.leave(d, 0) * value
     copies = exchange(solved, final, send_two, recv_two)
     some(groups // 2, groups)
     for copy in copies:
         copy.wait()
     rhs = jnp.concatenate([final[:, side].reshape(width, depth) for side in range(2)], axis=1)
-    answers = solve_group(rhs, coupling[0], width_ref, mixed_ref, depth_ref[...])
+    answers = solve_group(rhs, coupling[0], width_ref, mixed_ref, mixed_depth[...])
     for side in range(2):
         face_z[side] = answers[side]
+    edge_enter, edge_leave = ends_of(answers[0]), ends_of(answers[1])
+
+    def correct_ends(j, unused):
+        enter, leave = heights.enter(me, j)[:, 0:1], heights.leave(me, j)[:, 0:1]
+        ends[j] = ends[j] + enter * edge_enter + leave * edge_leave
+        return unused
 
     def correct(j, unused):
-        z = z_ref[j] + into[0, j] * face_z[0] + into[1, j] * face_z[1]
-        z_ref[j] = z
-        ends[j] = ends_of(z)
+        enter, leave = heights.enter(me, j), heights.leave(me, j)
+        z_ref[j] = z_ref[j] + enter * face_z[0] + leave * face_z[1]
+        store(j).start()
         return unused
 
-    lax.fori_loop(0, planes, correct, 0)
+    def finish_store(j, unused):
+        store(j).wait()
+        return unused
+
+    lax.fori_loop(0, planes, correct_ends, 0)
     copies = []
     for k in range(1, slabs):
         copy = pltpu.make_async_remote_copy(
@@ -266,16 +331,21 @@
         copy.start()
         copies.append(copy)
     gathered[slab] = ends[...]
+    lax.fori_loop(0, planes, correct, 0)
     for copy in copies:
         copy.wait()
+
+    def link(d, row, column):
+        return coupling[2] * depth_ref[d, row : row + 1, column : column + 1]
+
     zero = jnp.zeros((planes, width), F32)
     forward = [zero]
     for d in range(slabs - 1):
-        forward.append(gathered[d, :, 1] + links[0, d] * forward[d])
+        forward.append(gathered[d, :, 1] + link(d, size - 1, 0) * forward[d])
     backward = [zero] * slabs
     for d in range(slabs - 1, 0, -1):
         backward[d - 1] = (
-            gathered[d, :, 0] + links[1, d] * forward[d] + links[2, d] * backward[d]
+            gathered[d, :, 0] + link(d, 0, 0) * forward[d] + link(d, 0, size - 1) * backward[d]
         )
     carry_in, carry_next = forward[0], backward[0]
     for d in range(1, slabs):
@@ -283,12 +353,14 @@
         carry_next = jnp.where(slab == d, backward[d], carry_next)
     carry_ref[:, 0] = carry_in
     carry_ref[:, 1] = carry_next
-
-
-def finish_kernel(group, rho_ref, z_ref, carry_ref, edge_ref, out_ref):
+    lax.fori_loop(0, planes, finish_store, 0)
+
+
+def finish_kernel(group, coupling, rho_ref, z_ref, carry_ref, depth_ref, out_ref):
     width, depth = rho_ref.shape[1:]
-    in_high, in_low = split(edge_ref[0:1])
-    next_high, next_low = split(edge_ref[1:2])
+    slab, size = lax.axis_index("slab"), depth_ref.shape[1]
+    in_high, in_low = split(coupling[2] * depth_ref[slab, 0:1])
+    next_high, next_low = split(coupling[2] * depth_ref[slab, size - 1 : size])
     rhs = rows_of((in_high, in_high, in_low, next_high, next_high, next_low), depth)
     for g in range(group):
         a_high, a_low = split(carry_ref[g, 0:1])
@@ -297,37 +369,9 @@
         out_ref[g] = rho_ref[g] + z_ref[g] + dot(lhs, rhs, ((0,), (0,)))
 
 
-def height_tables(strength, planes, count):
-    root = (1.0 + 2.0 * strength + jnp.sqrt(1.0 + 4.0 * strength)) * 0.5
-    ratio = strength / root
-    log_ratio = jnp.log(ratio)
-
-    def tail(index):
-        return 1.0 - jnp.exp((2.0 * (index + 1.0)) * log_ratio)
-
-    def power(index):
-        return jnp.exp(index * log_ratio)
-
-    base = (jnp.arange(count, dtype=F32) * planes)[:, None]
-    j = jnp.arange(planes, dtype=F32)[None, :]
-    pivots = tail(base + j) / (root * tail(base + j + 1.0))
-    leave = power(planes - j) * tail(base + j) / tail(base + planes)
-    base3, j3, m3 = base[:, :, None], j[:, :, None], j[:, None, :]
-    distance = jnp.maximum(m3 - j3, 0.0)
-    terms = (
-        power(distance + m3 + 1.0)
-        * (tail(base3 + j3) / tail(base3 + m3))
-        * (tail(base3) / tail(base3 + m3 + 1.0))
-    )
-    enter = jnp.sum(jnp.where(m3 >= j3, terms, 0.0), axis=2)
-    through = power(float(planes)) * tail(base[:, 0]) / tail(base[:, 0] + planes)
-    return pivots, enter, leave, through
-
-
 def per_device(density, source, coupling, width_inverse, height_inverse, depth_inverse):
     planes, width, depth = density.shape
     pencils, slabs = lax.axis_size("pencil"), lax.axis_size("slab")
-    pencil, slab = lax.axis_index("pencil"), lax.axis_index("slab")
     size = depth_inverse.shape[1]
     group = 2
     smem = pl.BlockSpec(memory_space=pltpu.SMEM)
@@ -345,6 +389,8 @@
         return pl.BlockSpec(shape, lambda j: (0, j, 0, 0))
 
     vmem = pl.BlockSpec(memory_space=pltpu.VMEM)
+    hbm = pl.BlockSpec(memory_space=pl.ANY)
+    blocks = width_inverse.shape[0]
     dma = pltpu.SemaphoreType.DMA
     strip = (2, planes, 1, width)
     halo = pl.pallas_call(
@@ -362,14 +408,6 @@
         ),
     )(density)
 
-    pivots, enter, leave, through = height_tables(coupling[1], planes, pencils)
-    own_pivots = lax.dynamic_index_in_dim(pivots, pencil, 0, False)
-    into = jnp.stack(
-        [
-            lax.dynamic_index_in_dim(enter, pencil, 0, False),
-            lax.dynamic_index_in_dim(leave, pencil, 0, False),
-        ]
-    )
     share = width // pencils
     partial, faces = pl.pallas_call(
         lambda *refs: height_kernel(planes, group, *refs),
@@ -380,7 +418,6 @@
         ),
         in_specs=[
             smem,
-            smem,
             per_plane((group, width, depth)),
             per_plane((group, width, depth)),
             plane_pairs((2, group, 1, width)),
@@ -388,30 +425,8 @@
         out_specs=(whole((planes, width, depth)), whole((pencils, 2, share, depth))),
         scratch_shapes=[pltpu.VMEM((planes, width, depth), F32)],
         compiler_params=params,
-    )(coupling, own_pivots, density, source, halo)
-
-    w_high, w_low = split_outside(width_inverse)
-    mixed = jnp.concatenate(
-        [
-            jnp.concatenate([w_high, w_high], axis=2),
-            jnp.concatenate([w_low, jnp.zeros_like(w_low)], axis=2),
-        ],
-        axis=1,
-    )
-    matrix = lax.dynamic_index_in_dim(depth_inverse, slab, 0, False).T
-    d_high, d_low = split_outside(matrix)
-    depth_mixed = jnp.concatenate(
-        [
-            jnp.concatenate([d_high, d_low], axis=1),
-            jnp.concatenate([d_high, jnp.zeros_like(d_low)], axis=1),
-        ],
-        axis=0,
-    )
-    strength = coupling[2]
-    chain = jnp.stack([through, enter[:, 0], leave[:, 0]])
-    links = strength * jnp.stack(
-        [depth_inverse[:, size - 1, 0], depth_inverse[:, 0, 0], depth_inverse[:, 0, size - 1]]
-    )
+    )(coupling, density, source, halo)
+
     pieces = pltpu.VMEM((pencils, 2, share, depth), F32)
     local, carries = pl.pallas_call(
         lambda *refs: lines_kernel(group, pencils, slabs, *refs),
@@ -419,9 +434,13 @@
             jax.ShapeDtypeStruct((planes, width, depth), F32),
             jax.ShapeDtypeStruct((planes, 2, width), F32),
         ),
-        in_specs=[smem] * 4 + [vmem] * 5,
-        out_specs=(vmem, vmem),
+        in_specs=[smem, hbm, vmem, vmem, vmem],
+        out_specs=(hbm, vmem),
         scratch_shapes=[
+            pltpu.VMEM((planes, width, depth), F32),
+            pltpu.VMEM((planes, width, depth), F32),
+            pltpu.VMEM((blocks, 2 * size, 2 * size), BF16),
+            pltpu.VMEM((2 * size, 2 * size), BF16),
             pieces,
             pieces,
             pieces,
@@ -434,26 +453,28 @@
             dma((pencils - 1,)),
             dma((slabs - 1,)),
             dma((slabs - 1,)),
+            dma((planes // group,)),
+            dma((planes,)),
         ],
         compiler_params=pltpu.CompilerParams(
             vmem_limit_bytes=56 * 1024 * 1024, collective_id=1, has_side_effects=True
         ),
-    )(coupling, into, chain, links, partial, faces, width_inverse, mixed, depth_mixed)
-
-    edges = strength * jnp.stack([matrix[0], matrix[size - 1]])
+    )(coupling, partial, faces, width_inverse, depth_inverse)
+
     return pl.pallas_call(
         lambda *refs: finish_kernel(group, *refs),
         grid=(planes // group,),
         out_shape=jax.ShapeDtypeStruct((planes, width, depth), F32),
         in_specs=[
+            smem,
             per_plane((group, width, depth)),
             per_plane((group, width, depth)),
             per_plane((group, 2, width)),
-            whole((2, depth)),
+            whole(depth_inverse.shape),
         ],
         out_specs=per_plane((group, width, depth)),
         compiler_params=params,
-    )(density, local, carries, edges)
+    )(coupling, density, local, carries, depth_inverse)
 
 
 def solution(mesh):

time: 106 us -> 85.7 us (0.81)
  Pallas kernels: 93.7 us -> 85 us
  other arithmetic: 5.66 us -> 0 us
  local copies, waits for them, and re-layouts: 4.07 us -> 0 us
  between operations: 2.32 us -> 0.02 us
    pallas_call x1, Pallas kernels: 57.8 us -> 49.4 us  [per_device(): pl.pallas_call(lambda *refs: lines_kernel(group, pencils, slabs, *refs),...]
    slice x5 -> x0, local copies, waits for them, and re-layouts: 2.63 us -> none  [the longest x1 1.4 us: per_device(): strength = coupling[2]]
    mul x3 -> x0, other arithmetic: 2.47 us -> none  [the longest x1 1.24 us: per_device(): strength * jnp.stack([depth_inverse[:, size - 1, 0], depth_inverse[:, 0,...]
    concatenate x2 -> x0, other arithmetic: 1.59 us -> none  [the longest x1 0.94 us: per_device(): jnp.concatenate([jnp.concatenate([w_high, w_high], axis=2), jnp.concatena...]
    another operation x2 -> x0, other arithmetic: 1.18 us -> none  [the longest x1 0.6 us: per_device(): jnp.stack([lax.dynamic_index_in_dim(enter, pencil, 0, False), lax.dynamic...]
where the time goes in v3:
time: 85.7 us; the launch traced here: 85 us
  Pallas kernels  85 us (99%)
    pallas_call x1, Pallas kernels, per_device(): pl.pallas_call(lambda *refs: lines_kernel(group, pencils, slabs, *refs),...  49.4 us
    pallas_call x1, Pallas kernels, per_device(): pl.pallas_call(lambda *refs: height_kernel(planes, group, *refs), grid=(p...  15.1 us
    pallas_call x1, Pallas kernels, per_device(): pl.pallas_call(lambda *refs: finish_kernel(group, *refs), grid=(planes //...  10.6 us
    pallas_call x1, Pallas kernels, per_device(): pl.pallas_call(lambda *refs: ends_kernel(slabs, 4, *refs), grid=(planes /...  9.92 us

profile of v3, /device:TPU:27, one launch (start us, length us, event | category | flops | bytes accessed | tf_op | source)
XLA Modules:
  0.0 85.0 jit_solution(13938588698687344015)
XLA Ops:
  0.0 9.9 %shard_map.55.refs_3_ = f32[2,16,1,768]{3,2,1,0:T(1,128)} custom-call(f32[16,768,128]{2,1,0:T(8,128)} %refs_1_.3), custom_call_target="tpu_custom_call" | custom-call | tf_op jit(solution)/shard_map/pallas_call | solution.py:396
  9.9 15.1 %shard_map.56 = (f32[16,768,128]{2,1,0:T(8,128)}, f32[8,2,96,128]{3,2,1,0:T(8,128)}) custom-call(f32[3]{0:T(128)} %refs_0_.7, f32[16,768,128]{2,1,0:T(8,128)} %refs_1_.3, f32[16,768,128]{2,1,0:T(8,128)} %refs_2_.1, f32[2,16,1,768]{3,2,1,0:T(1,128)} %shard_map.55.refs_3_), custom_call_target="tpu_custom_call" | custom-call | tf_op jit(solution)/shard_map/pallas_call | solution.py:412
  25.0 49.4 %shard_map.57 = (f32[16,768,128]{2,1,0:T(8,128)}, f32[16,2,768]{2,1,0:T(2,128)}) custom-call(f32[3]{0:T(128)} %refs_0_.7, f32[16,768,128]{2,1,0:T(8,128)} %get-tuple-element.9.refs_1_, f32[8,2,96,128]{3,2,1,0:T(8,128)} %get-tuple-element.10.refs_2_, f32[6,128,128]{2,1,0:T(8,128)} %refs_3_.1, f32[4,128,128]{2,1,0:T(8,128)} %refs_4_.3), custom_call_target="tpu_custom_call" | custom-call | tf_op jit(solution)/shard_map/pallas_call | solution.py:431
  74.4 10.6 %shard_map.58 = f32[16,768,128]{2,1,0:T(8,128)} custom-call(f32[3]{0:T(128)} %refs_0_.7, f32[16,768,128]{2,1,0:T(8,128)} %refs_1_.3, f32[16,768,128]{2,1,0:T(8,128)} %get-tuple-element.11.refs_2_, f32[16,2,768]{2,1,0:T(2,128)} %get-tuple-element.12.refs_3_, f32[4,128,128]{2,1,0:T(8,128)} %refs_4_.3), custom_call_target="tpu_custom_call" | custom-call | tf_op jit(solution)/shard_map/pallas_call | solution.py:464
